TPU v7x, 32 devices: a whole 2x2x4 slice. The times are simulated.
32 devices in a mesh: dp: 16 (over z, y, x), mp: 2 (over core).
Axes of the slice: x: 2, y: 2, z: 4, core: 2. Of those that a mesh axis runs over, the one named last changes fastest.
Arguments:
- patches: bfloat16 [8192, 3200], P(('dp', 'mp')), may hold values from -120 to 120
- ln_gain: bfloat16 [3200], replicated, may hold values from 0.099609375 to 1.8984375
- ln_bias: bfloat16 [3200], replicated, may hold values from -3 to 3
- w_proj: bfloat16 [3200, 4096], P(None, 'mp'), may hold values from -0.109375 to 0.109375
- proj_bias: bfloat16 [4096], P('mp'), may hold values from -3 to 3
- rms_gain: bfloat16 [4096], replicated, may hold values from 0.099609375 to 1.8984375
- w_qkv: bfloat16 [4096, 3072], P(None, 'mp'), may hold values from -4 to 4
- image_counts: int32 [64, 8], replicated, may hold values from 1 to 16, as said below
- source_shift: int32 [32], replicated, may hold values from 0 to 15, as said below
Outputs:
- attended: bfloat16 [8192, 2048], P('dp', 'mp')
Inputs may be any that keep to these rules, and one draw needn't show every extreme that they name: `image_counts`: row g holds the counts of the 8 images of tile g. In every draw all images of the tiles of some dp index hold 16 tokens. No value stands more than 2 times in source_shift, and some value stands exactly 2 times.
All inputs are finite; a program needn't handle non-finite values.
Results may differ from a plain program's by a relative error of at most 0.012.
Values may be sent and summed in bfloat16 or wider, within the bound.
A program may use at most 128 MiB of HBM per device.

v0:
```python
import jax
import jax.numpy as jnp
from jax import lax
from jax.sharding import PartitionSpec as P

HEAD_SIZE = 128
TILE = 128
QUERY_PER_KEY = 4


norm_epsilon = 1e-05
rms_epsilon = 1e-05
rotary_base = 500000.0


def layer_norm(row_block, gain_vec, bias_vec):
    values = row_block.astype(jnp.float32)
    row_mean = jnp.mean(values, axis=-1, keepdims=True)
    centred = values - row_mean
    row_var = jnp.mean(centred * centred, axis=-1, keepdims=True)
    scaled = centred * lax.rsqrt(row_var + norm_epsilon) * gain_vec.astype(jnp.float32)
    return (scaled + bias_vec.astype(jnp.float32)).astype(jnp.bfloat16)


def rotary(values, cos_table, sine_table):
    half_width = values.shape[-1] // 2
    turned = jnp.concatenate([-values[..., half_width:], values[..., :half_width]], axis=-1)
    return values * cos_table + turned * sine_table


def attend(queries, key_rows, value_rows, segment):
    tile_count = queries.shape[0] // TILE
    groups = queries.shape[1]
    query_f = queries.reshape(tile_count, TILE, groups, QUERY_PER_KEY, HEAD_SIZE).astype(
        jnp.float32
    )
    key_f = key_rows.reshape(tile_count, TILE, groups, HEAD_SIZE).astype(jnp.float32)
    value_f = value_rows.reshape(tile_count, TILE, groups, HEAD_SIZE).astype(jnp.float32)
    scores = jnp.einsum("tqhgd,tkhd->thgqk", query_f, key_f) * HEAD_SIZE ** (-0.5)
    segments = segment.reshape(tile_count, TILE)
    position = jnp.arange(TILE, dtype=jnp.int32)
    allowed = (position[None, :, None] >= position[None, None, :]) & (
        segments[:, :, None] == segments[:, None, :]
    )
    scores = jnp.where(allowed[:, None, None], scores, -1e30)
    row_max = jnp.max(scores, axis=-1, keepdims=True)
    weights = jnp.exp(scores - row_max)
    probabilities = (weights / jnp.sum(weights, axis=-1, keepdims=True)).astype(jnp.bfloat16)
    attended = jnp.einsum("thgqk,tkhd->tqhgd", probabilities.astype(jnp.float32), value_f)
    return attended.reshape(tile_count * TILE, groups * QUERY_PER_KEY * HEAD_SIZE)


def finish(hidden, live_flat, segment, rms_gain, w_qkv):
    row_total = hidden.shape[0]
    widened = hidden.astype(jnp.float32)
    mean_square = jnp.mean(widened * widened, axis=-1, keepdims=True)
    rms_normed = (
        widened * lax.rsqrt(mean_square + rms_epsilon) * rms_gain.astype(jnp.float32)
    ).astype(jnp.bfloat16)
    projections = jnp.dot(rms_normed, w_qkv, preferred_element_type=jnp.float32)
    groups = w_qkv.shape[1] // ((QUERY_PER_KEY + 2) * HEAD_SIZE)
    projections = projections.reshape(row_total, groups, QUERY_PER_KEY + 2, HEAD_SIZE)
    position = (jnp.arange(row_total, dtype=jnp.int32) % TILE).astype(jnp.float32)
    frequency = rotary_base ** (
        -(jnp.arange(HEAD_SIZE // 2, dtype=jnp.float32) * (2.0 / HEAD_SIZE))
    )
    angles = position[:, None] * frequency[None, :]
    cos_table = jnp.concatenate([jnp.cos(angles), jnp.cos(angles)], axis=-1)[:, None, None, :]
    sine_table = jnp.concatenate([jnp.sin(angles), jnp.sin(angles)], axis=-1)[:, None, None, :]
    queries = rotary(projections[:, :, :QUERY_PER_KEY], cos_table, sine_table).astype(jnp.bfloat16)
    key_rows = rotary(
        projections[:, :, QUERY_PER_KEY], cos_table[:, :, 0], sine_table[:, :, 0]
    ).astype(jnp.bfloat16)
    value_rows = projections[:, :, QUERY_PER_KEY + 1].astype(jnp.bfloat16)
    attended = attend(queries, key_rows, value_rows, segment).astype(jnp.bfloat16)
    return jnp.where(live_flat[:, None], attended, jnp.zeros_like(attended))


def deliver(blocks, source_shift, senders, my_index):
    img_dev = blocks.shape[0]
    img_most = blocks.shape[1]
    images = jnp.arange(img_dev, dtype=jnp.int32)
    pair_slots = (img_dev + senders - 1) // senders
    same_shift = (source_shift[:, None] == source_shift[None, :]) & (
        images[None, :] < images[:, None]
    )
    slot_rank = jnp.sum(same_shift.astype(jnp.int32), axis=1)
    targets = jnp.mod(my_index - source_shift, senders)
    outbox = jnp.zeros((senders * pair_slots, img_most, blocks.shape[2]), jnp.bfloat16)
    outbox = outbox.at[targets * pair_slots + slot_rank].set(blocks)
    in_box = lax.all_to_all(
        outbox.reshape(senders, pair_slots * img_most, blocks.shape[2]),
        "dp",
        split_axis=0,
        concat_axis=0,
        tiled=True,
    )
    anchors = jnp.mod(my_index + source_shift, senders)
    arrived = jnp.take(
        in_box.reshape(senders * pair_slots, img_most, blocks.shape[2]),
        anchors * pair_slots + slot_rank,
        axis=0,
    )
    return arrived


def local(
    patches, ln_gain, ln_bias, w_proj, proj_bias, rms_gain, w_qkv, image_counts, source_shift
):
    senders = lax.axis_size("dp")
    my_index = lax.axis_index("dp")
    normed_half = layer_norm(patches, ln_gain, ln_bias)
    normed = lax.all_gather(normed_half, "mp", axis=0, tiled=True)
    tok_rows = normed.shape[0]
    pre_act = jnp.dot(normed, w_proj, preferred_element_type=jnp.float32) + proj_bias.astype(
        jnp.float32
    )
    projected = jax.nn.gelu(pre_act, approximate=False).astype(jnp.bfloat16)
    img_dev = source_shift.shape[0]
    tiles_dev = tok_rows // TILE
    img_tile = img_dev // tiles_dev
    img_most = TILE // img_tile
    per_dest = image_counts.reshape(senders, img_dev)
    images = jnp.arange(img_dev, dtype=jnp.int32)
    targets = jnp.mod(my_index - source_shift, senders)
    sent_counts = per_dest[targets, images]
    starts = jnp.cumsum(sent_counts) - sent_counts
    inside = jnp.arange(img_most, dtype=jnp.int32)
    pick_rows = jnp.minimum(starts[:, None] + inside[None, :], tok_rows - 1).reshape(-1)
    blocks = jnp.take(projected, pick_rows, axis=0).reshape(img_dev, img_most, projected.shape[1])
    arrived = deliver(blocks, source_shift, senders, my_index)
    my_tiles = lax.dynamic_slice_in_dim(image_counts, my_index * tiles_dev, tiles_dev, 0)
    slot_ends = jnp.cumsum(my_tiles, axis=1)
    offsets = slot_ends - my_tiles
    position = jnp.arange(TILE, dtype=jnp.int32)
    slot_index = jnp.sum(
        (position[None, :, None] >= slot_ends[:, None, :]).astype(jnp.int32), axis=2
    )
    live_rows = slot_index < img_tile
    clipped = jnp.minimum(slot_index, img_tile - 1)
    inside_tile = position[None, :] - jnp.take_along_axis(offsets, clipped, axis=1)
    image_k = jnp.arange(tiles_dev, dtype=jnp.int32)[:, None] * img_tile + clipped
    pick_back = jnp.where(live_rows, image_k * img_most + inside_tile, 0).reshape(-1)
    placed = jnp.take(arrived.reshape(img_dev * img_most, arrived.shape[2]), pick_back, axis=0)
    live_flat = live_rows.reshape(-1)
    hidden_half = jnp.where(live_flat[:, None], placed, jnp.zeros_like(placed))
    hidden = lax.all_gather(hidden_half, "mp", axis=1, tiled=True)
    return finish(hidden, live_flat, slot_index.reshape(-1), rms_gain, w_qkv)


def solution(mesh):
    in_specs = (
        P(("dp", "mp"), None),
        P(),
        P(),
        P(None, "mp"),
        P("mp"),
        P(),
        P(None, "mp"),
        P(),
        P(),
    )
    out_specs = P("dp", "mp")
    return jax.shard_map(local, mesh=mesh, in_specs=in_specs, out_specs=out_specs, check_vma=False)
```

profile of v0, /device:TPU:0, one launch (start us, length us, event | category | flops | bytes accessed | tf_op | source)
XLA Modules:
  0.0 170.7 jit_solution(5769943672025603418)
XLA Ops:
  6.6 1.8 %convert_reduce_fusion = f32[256]{0:T(256)S(1)} fusion(bf16[256,3200]{1,0:T(8,128)(2,1)} %param.11), kind=kLoop, calls=%fused_computation.35 | loop fusion | flops 1638144 | bytes 1639424 | tf_op jit(solution)/shard_map/reduce_sum | solution.py:18
  8.4 2.0 %fusion.20 = f32[256]{0:T(256)S(1)} fusion(bf16[256,3200]{1,0:T(8,128)(2,1)} %param.11, f32[256]{0:T(256)S(1)} %broadcast_multiply_fusion), kind=kLoop, calls=%fused_computation.38 | loop fusion | flops 3276544 | bytes 1640448 | tf_op jit(solution)/shard_map/reduce_sum | solution.py:20
  11.9 2.0 %fusion.23 = bf16[256,3200]{1,0:T(8,128)(2,1)} fusion(bf16[256,3200]{1,0:T(8,128)(2,1)S(1)} %copy-done, f32[3200]{0:T(1024)S(1)} %convert_element_type.87, f32[3200]{0:T(1024)S(1)} %convert_element_type.86, f32[256]{0:T(256)S(1)} %add_rsqrt_fusion.1, f32[256]{0:T(256)S(1)} %broadcast_multiply_fusion), kind=kLoop, calls=%fused_computation.41 | loop fusion | flops 4915200 | bytes 3304448 | tf_op jit(solution)/shard_map/convert_element_type | solution.py:22
  15.4 13.6 %all-gather.3.cloned.1.call-done = bf16[512,3200]{1,0:T(8,128)(2,1)} async-done(((bf16[256,3200]{1,0:T(8,128)(2,1)}), bf16[512,3200]{1,0:T(8,128)(2,1)}) %all-gather.3.cloned.1.call-update) | async-done | bytes 3276816 | tf_op jit(solution)/shard_map/all_gather | solution.py:113
  29.1 19.8 %fusion.6 = bf16[512,2048]{1,0:T(8,128)(2,1)S(1)} fusion(bf16[512,3200]{1,0:T(8,128)(2,1)} %all-gather.3.cloned.1.call-done, bf16[3200,2048]{1,0:T(8,128)(2,1)} %param.14, f32[2048]{0:T(1024)S(1)} %convert_element_type.89), kind=kOutput, calls=%fused_computation.15 | convolution fusion | flops 6780092416 | bytes 18489344 | tf_op jit(solution)/shard_map/dot_general | solution.py:115
  48.8 3.3 %gather_fusion.3 = bf16[512,2048]{1,0:T(8,128)(2,1)} fusion(bf16[512,2048]{1,0:T(8,128)(2,1)S(1)} %fusion.6, s32[1024]{0:T(1024)S(1)} %pad_clamp_fusion.2), kind=kCustom, calls=%fused_computation.clone | custom fusion | bytes 4196352 | tf_op jit(solution)/shard_map/jit(_take)/gather | solution.py:130
  52.2 1.8 %broadcast_select_fusion = bf16[512,2048]{1,0:T(8,128)(2,1)S(1)} fusion(bf16[512,2048]{1,0:T(8,128)(2,1)} %gather_fusion.3, pred[512]{0:T(512)(128)(4,1)S(1)} %compare_and_fusion.2), kind=kLoop, calls=%fused_computation.51 | loop fusion | flops 1048576 | bytes 4194816 | tf_op jit(solution)/shard_map/jit(_take)/select_n | solution.py:130
  54.0 1.6 broadcast_in_dim.106
  55.6 5.4 %scatter_fusion = bf16[32,16,2048]{2,1,0:T(8,128)(2,1)} fusion(bf16[32,16,2048]{2,1,0:T(8,128)(2,1)} %broadcast_in_dim.106, s32[32]{0:T(128)S(1)} %compare_select_fusion.5, bf16[32,16,2048]{2,1,0:T(8,128)(2,1)S(1)} %bitcast.72), kind=kCustom, calls=%fused_computation.5 | custom fusion | bytes 6291584 | tf_op jit(solution)/shard_map/scatter | solution.py:90
  61.1 6.8 %all-to-all-start = ((bf16[16,32,2048]{2,1,0:T(8,128)(2,1)}), bf16[16,32,2048]{2,1,0:T(8,128)(2,1)S(1)}, u32[]{:S(2)}, u32[]{:S(2)}) async-start(bf16[16,32,2048]{2,1,0:T(8,128)(2,1)} %bitcast.10), calls=%async_computation | async-start | bytes 4194304 | tf_op jit(solution)/shard_map/all_to_all | solution.py:91
  68.6 2.6 %gather_fusion.2 = s32[512]{0:T(512)S(1)} fusion(s32[4,8]{0,1:T(8,128)S(1)} %fusion.86, s32[512]{0:T(512)S(1)} %fusion.52), kind=kCustom, calls=%fused_computation.4 | custom fusion | bytes 8192 | tf_op jit(solution)/shard_map/jit(take_along_axis)/gather | solution.py:141
  71.4 39.7 %all-to-all-done = bf16[16,32,2048]{2,1,0:T(8,128)(2,1)S(1)} async-done(((bf16[16,32,2048]{2,1,0:T(8,128)(2,1)}), bf16[16,32,2048]{2,1,0:T(8,128)(2,1)S(1)}, u32[]{:S(2)}, u32[]{:S(2)}) %all-to-all-start) | async-done | bytes 2097184 | tf_op jit(solution)/shard_map/all_to_all | solution.py:91
  111.1 2.0 %gather_fusion.1 = bf16[32,16,2048]{2,1,0:T(8,128)(2,1)} fusion(bf16[32,16,2048]{2,1,0:T(8,128)(2,1)S(1)} %bitcast.73, s32[1024]{0:T(1024)S(1)} %pad_clamp_fusion.1), kind=kCustom, calls=%fused_computation.3 | custom fusion | bytes 4194432 | tf_op jit(solution)/shard_map/jit(_take)/gather | solution.py:99
  113.1 1.8 %bitcast_select_fusion.1 = bf16[512,2048]{1,0:T(8,128)(2,1)S(1)} fusion(bf16[32,16,2048]{2,1,0:T(8,128)(2,1)} %gather_fusion.1, pred[512]{0:T(512)(128)(4,1)S(1)} %broadcast_in_dim.104), kind=kLoop, calls=%fused_computation.47 | loop fusion | flops 1048576 | bytes 4194816 | tf_op jit(solution)/shard_map/jit(_take)/select_n | solution.py:99
  115.0 3.3 %gather_fusion.4 = bf16[512,2048]{1,0:T(8,128)(2,1)} fusion(bf16[512,2048]{1,0:T(8,128)(2,1)S(1)} %bitcast_select_fusion.1, s32[1024]{0:T(1024)S(1)} %pad_clamp_fusion), kind=kCustom, calls=%fused_computation.1.clone | custom fusion | bytes 4196352 | tf_op jit(solution)/shard_map/jit(_take)/gather | solution.py:144
  118.3 3.3 %select_select_fusion = bf16[512,2048]{1,0:T(8,128)(2,1)} fusion(bf16[512,2048]{1,0:T(8,128)(2,1)} %gather_fusion.4, pred[512]{0:T(512)(128)(4,1)S(1)} %get-tuple-element.6, pred[512]{0:T(512)(128)(4,1)S(1)} %compare_bitcast_fusion), kind=kLoop, calls=%fused_computation.48 | loop fusion | flops 2097152 | bytes 4195328 | tf_op jit(solution)/shard_map/jit(_where)/select_n | solution.py:146
  122.3 1.0 multiply_cosine_fusion
  123.3 1.0 pad_maximum_fusion
  124.4 15.8 %all-gather.5.cloned.1.call-done = bf16[512,4096]{1,0:T(8,128)(2,1)} async-done(((bf16[512,2048]{1,0:T(8,128)(2,1)}), bf16[512,4096]{1,0:T(8,128)(2,1)}) %all-gather.5.cloned.1.call-update) | async-done | bytes 4194320 | tf_op jit(solution)/shard_map/all_gather | solution.py:147
  140.2 3.2 %fusion.1 = f32[512]{0:T(512)S(1)} fusion(bf16[512,4096]{1,0:T(8,128)(2,1)} %all-gather.5.cloned.1.call-done), kind=kLoop, calls=%fused_computation.9 | loop fusion | flops 6290944 | bytes 4196352 | tf_op jit(solution)/shard_map/reduce_sum | solution.py:56
  143.7 9.7 %fusion.7 = f32[512,1536]{0,1:T(8,128)S(1)} fusion(bf16[4096,1536]{1,0:T(8,128)(2,1)} %param.17, bf16[512,4096]{1,0:T(8,128)(2,1)S(1)} %copy-done.1, f32[4096]{0:T(1024)S(1)} %convert_element_type.92, f32[512]{0:T(512)S(1)} %add_rsqrt_fusion), kind=kOutput, calls=%fused_computation.16 | convolution fusion | flops 6450839552 | bytes 19941376 | tf_op jit(solution)/shard_map/dot_general | solution.py:60
  155.9 3.3 %fusion.78 = (f32[4,2,4,128]{3,2,1,0:T(4,128)S(1)}, f32[4,2,4,128,128]{3,4,2,1,0:T(8,128)}) fusion(pred[4,128,128]{1,2,0:T(8,128)(4,1)S(1)} %compare_and_fusion, bf16[4,128,2,4,128]{4,1,0,3,2:T(8,128)(2,1)S(1)} %bitcast.78, f32[4,128,2,64]{3,1,0,2:T(8,128)S(1)} %bitcast.80, f32[4,128,2,64]{3,1,0,2:T(8,128)S(1)} %bitcast.79, ...), kind=kOutput, calls=%fused_computation.146 | convolution fusion | flops 136970368 | bytes 4800512 | tf_op jit(solution)/shard_map/sub | solution.py:47
  159.2 2.1 %fusion.27 = bf16[4,128,2,4,128]{1,4,3,2,0:T(8,128)(2,1)S(1)} fusion(f32[4,2,4,128,128]{3,4,2,1,0:T(8,128)} %get-tuple-element.23, f32[4,2,4,128]{3,2,1,0:T(4,128)S(1)} %get-tuple-element.22, bf16[4,128,2,128,1]{3,1,0,2,4:T(8,128)(2,1)S(1)} %bitcast.82), kind=kOutput, calls=%fused_computation.54 | convolution fusion | flops 135790592 | bytes 3424256 | tf_op jit(solution)/shard_map/thgqk,tkhd->tqhgd/dot_general | solution.py:49
  162.8 1.1 broadcast_select_fusion.1
  (71 shorter events, 8.9 us)
Async XLA Ops:
  6.5 5.3 %copy-start = (bf16[256,3200]{1,0:T(8,128)(2,1)S(1)}, bf16[256,3200]{1,0:T(8,128)(2,1)}, u32[]{:S(2)}) copy-start(bf16[256,3200]{1,0:T(8,128)(2,1)} %param.11) | copy-start | bytes 4915204
  6.5 7.3 %copy-start.2 = (s32[64,8]{0,1:T(8,128)S(1)}, s32[64,8]{0,1:T(8,128)}, u32[]{:S(2)}) copy-start(s32[64,8]{0,1:T(8,128)} %param.18) | copy-start | bytes 6148
  6.5 7.5 %copy-start.5 = (s32[32]{0:T(128)S(1)}, s32[32]{0:T(128)}, u32[]{:S(2)}) copy-start(s32[32]{0:T(128)} %param.19) | copy-start | bytes 388
  6.5 8.7 %copy-start.4 = (bf16[2048]{0:T(1024)(128)(2,1)S(1)}, bf16[2048]{0:T(1024)(128)(2,1)}, u32[]{:S(2)}) copy-start(bf16[2048]{0:T(1024)(128)(2,1)} %param.15) | copy-start | bytes 12292
  6.5 22.5 %all-gather.3.cloned.1.call-start = ((), (), s32[]{:S(2)}) async-start(), calls=%async_computation.1 | async-start | bytes 4915200 | tf_op jit(solution)/shard_map/all_gather | solution.py:113
  61.1 50.0 %all-to-all-start = ((bf16[16,32,2048]{2,1,0:T(8,128)(2,1)}), bf16[16,32,2048]{2,1,0:T(8,128)(2,1)S(1)}, u32[]{:S(2)}, u32[]{:S(2)}) async-start(bf16[16,32,2048]{2,1,0:T(8,128)(2,1)} %bitcast.10), calls=%async_computation | async-start | bytes 4194304 | tf_op jit(solution)/shard_map/all_to_all | solution.py:91
  67.9 72.3 %all-gather.5.cloned.1.call-start = ((), (), s32[]{:S(2)}) async-start(), calls=%async_computation.2 | async-start | bytes 6291456 | tf_op jit(solution)/shard_map/all_gather | solution.py:147
  118.3 3.3 %copy-start.3 = (bf16[4096]{0:T(1024)(128)(2,1)S(1)}, bf16[4096]{0:T(1024)(128)(2,1)}, u32[]{:S(2)}) copy-start(bf16[4096]{0:T(1024)(128)(2,1)} %param.16) | copy-start | bytes 24580
  140.2 3.4 %copy-start.1 = (bf16[512,4096]{1,0:T(8,128)(2,1)S(1)}, bf16[512,4096]{1,0:T(8,128)(2,1)}, u32[]{:S(2)}) copy-start(bf16[512,4096]{1,0:T(8,128)(2,1)} %all-gather.5.cloned.1.call-done) | copy-start | bytes 12582916
Sparse Core Ops, SparseCore 0:
  14.0 15.0 all-gather.2
  121.7 18.4 all-gather.4
where the time goes:
time: 171 us
  waiting for transfers between devices  69.1 us (40%)
  matrix products  34.8 us (20%)
  local copies, waits for them, and re-layouts  23 us (13%)
  other arithmetic  23 us (13%)
  between operations  13.7 us (8%)
  starting transfers between devices  7.05 us (4%)
    all_to_all x1, waiting for transfers between devices, deliver(): lax.all_to_all(outbox.reshape(senders, pair_slots * img_most, blocks.shap...  39.7 us
    dot_general x1, matrix products, local(): jnp.dot(normed, w_proj, preferred_element_type=jnp.float32)  19.8 us
    all_gather x1, waiting for transfers between devices, local(): hidden = lax.all_gather(hidden_half, 'mp', axis=1, tiled=True)  15.8 us
    all_gather x1, waiting for transfers between devices, local(): normed = lax.all_gather(normed_half, 'mp', axis=0, tiled=True)  13.6 us
    dot_general x1, matrix products, finish(): projections = jnp.dot(rms_normed, w_qkv, preferred_element_type=jnp.float32)  9.67 us
    all_to_all x1, starting transfers between devices, deliver(): lax.all_to_all(outbox.reshape(senders, pair_slots * img_most, blocks.shap...  6.79 us
    scatter x1, local copies, waits for them, and re-layouts, deliver(): outbox = outbox.at[targets * pair_slots + slot_rank].set(blocks)  5.41 us
  transfers between devices with their start and end apart: 3, of which 3 were waited for; matrix products, arithmetic and copies ran while one was open for 4% of the time, Pallas kernels for 0%

commit v1 on v0

v1 whole, which is shorter than its diff:
```python
import functools

import jax
import jax.numpy as jnp
import numpy as np
from jax import lax
from jax.experimental import pallas as pl
from jax.experimental.pallas import tpu as pltpu
from jax.sharding import PartitionSpec as P

HEAD_SIZE = 128
TILE = 128
QUERY_PER_KEY = 4
COL_TILE = 256
CHUNK = 256

norm_epsilon = 1e-05
rms_epsilon = 1e-05
rotary_base = 500000.0

F32 = jnp.float32
BF16 = jnp.bfloat16
MESH = pl.DeviceIdType.MESH


def shift_order(senders):
    return sorted(range(senders), key=lambda v: (abs(v - senders // 2), v))


def rotary_parts():
    frequency = np.float32(rotary_base) ** (
        -(np.arange(HEAD_SIZE // 2, dtype=np.float32) * np.float32(2.0 / HEAD_SIZE))
    )
    angles = np.arange(TILE, dtype=np.float32)[:, None] * frequency[None, :].astype(np.float32)
    cos = np.cos(angles.astype(np.float64)).astype(np.float32)
    sin = np.sin(angles.astype(np.float64)).astype(np.float32)
    parts = []
    for table in (np.concatenate([cos, cos], 1), np.concatenate([-sin, sin], 1)):
        rest = table
        for _ in range(3):
            term = rest.astype(jnp.bfloat16)
            parts.append(term)
            rest = rest - term.astype(np.float32)
    return np.concatenate(parts, axis=1)


def gelu(v):
    return 0.5 * v * (1.0 + lax.erf(v * np.float32(0.5**0.5)))


def iota(shape, axis):
    return lax.broadcasted_iota(jnp.int32, shape, axis)


def lane_sum(x):
    return jnp.sum(x, axis=1, keepdims=True)


def kernel(
    senders,
    order,
    patches,
    ln_gain,
    ln_bias,
    proj_bias,
    rms_gain,
    per_dest,
    shift_col,
    table,
    w_proj,
    w_qkv,
    out,
    w1,
    w2,
    normed,
    picked,
    hidden,
    rms_normed,
    proj,
    outbox,
    inbox,
    w1_sem,
    w2_sem,
    norm_sems,
    hid_send,
    hid_recv,
    a2a_send,
    a2a_recv,
):
    me = lax.axis_index("dp")
    core = lax.axis_index("mp")
    peer = 1 - core
    half, d_vit = patches.shape
    rows = 2 * half
    box_rows = outbox.shape[0]
    block = box_rows // senders
    images = shift_col.shape[0]
    tiles_dev = rows // TILE
    img_tile = images // tiles_dev
    img_most = TILE // img_tile
    pair_slots = block // img_most
    chunks = box_rows // CHUNK
    half_cols = w_proj.shape[1]
    qkv_cols = w_qkv.shape[1]
    groups = qkv_cols // ((QUERY_PER_KEY + 2) * HEAD_SIZE)
    tiles1 = half_cols // COL_TILE
    tiles2 = qkv_cols // COL_TILE

    barrier = pltpu.get_barrier_semaphore()
    pl.semaphore_signal(barrier, inc=1, device_id={"mp": peer}, device_id_type=MESH)
    for v in range(1, senders):
        pl.semaphore_signal(
            barrier, inc=1, device_id={"dp": lax.rem(me + v, senders)}, device_id_type=MESH
        )

    def w1_copy(j):
        cols = pl.ds(pl.multiple_of(j * COL_TILE, COL_TILE), COL_TILE)
        return pltpu.make_async_copy(w_proj.at[:, cols], w1.at[:, cols], w1_sem.at[j])

    def w2_copy(j):
        cols = pl.ds(pl.multiple_of(j * COL_TILE, COL_TILE), COL_TILE)
        return pltpu.make_async_copy(w_qkv.at[:, cols], w2.at[:, cols], w2_sem.at[j])

    for j in range(tiles1):
        w1_copy(j).start()
    for j in range(tiles2):
        w2_copy(j).start()

    gain_f = ln_gain[...].astype(F32)
    bias_f = ln_bias[...].astype(F32)
    base = pl.multiple_of(core * half, half)

    @pl.loop(0, half // 16)
    def _(r):
        at = pl.ds(pl.multiple_of(r * 16, 16), 16)
        values = patches[at, :].astype(F32)
        centred = values - jnp.mean(values, axis=-1, keepdims=True)
        variance = jnp.mean(centred * centred, axis=-1, keepdims=True)
        scaled = centred * lax.rsqrt(variance + norm_epsilon) * gain_f + bias_f
        normed[pl.ds(pl.multiple_of(base + r * 16, 16), 16), :] = scaled.astype(BF16)

    pl.semaphore_wait(barrier, senders)

    mine = normed.at[pl.ds(base, half)]
    norm_copy = pltpu.make_async_remote_copy(
        src_ref=mine,
        dst_ref=mine,
        send_sem=norm_sems.at[0],
        recv_sem=norm_sems.at[1],
        device_id={"mp": peer},
        device_id_type=MESH,
    )
    norm_copy.start()

    sq = (images, images)
    k_at, l_at = iota(sq, 0), iota(sq, 1)
    eye = k_at == l_at
    before = l_at < k_at
    same_tile = (k_at // img_tile) == (l_at // img_tile)

    def to_row(col):
        return jnp.sum(jnp.where(eye, col, 0), axis=0, keepdims=True)

    shift = shift_col[...]
    dest = me - shift
    dest = jnp.where(dest < 0, dest + senders, dest)
    counts_to = jnp.zeros(sq, jnp.int32)
    place = jnp.zeros((images, 1), jnp.int32)
    for v in range(senders):
        counts_to = jnp.where(dest == v, per_dest[v : v + 1, :], counts_to)
        place = jnp.where(shift == order[v], v, place)
    sent_row = jnp.sum(jnp.where(eye, counts_to, 0), axis=0, keepdims=True)
    starts = lane_sum(jnp.where(before, sent_row, 0))
    far_offset = lane_sum(jnp.where(before & same_tile, counts_to, 0))
    shift_row = to_row(shift)
    rank = lane_sum(jnp.where(before & (shift_row == shift), 1, 0))
    slot_row = to_row(place * pair_slots + rank)
    starts_row = to_row(starts)
    far_row = to_row(far_offset)

    dest_at = iota(per_dest.shape, 0)
    my_row = jnp.sum(jnp.where(dest_at == me, per_dest[...], 0), axis=0, keepdims=True)
    my_offset = lane_sum(jnp.where(before & same_tile, my_row, 0))
    my_off_row = to_row(my_offset)

    box_at = (CHUNK, images)

    def of_chunk(c):
        row_at = iota(box_at, 0) + c * CHUNK
        hit = slot_row == row_at // img_most
        inside = (iota((CHUNK, 1), 0) + c * CHUNK) % img_most
        src = lane_sum(jnp.where(hit, starts_row, 0)) + inside
        pos = lane_sum(jnp.where(hit, far_row, 0)) + inside
        return src, pos

    def copy_hidden(c):
        ref = hidden.at[core, pl.ds(c * CHUNK, CHUNK)]
        return pltpu.make_async_remote_copy(
            src_ref=ref,
            dst_ref=ref,
            send_sem=hid_send.at[c],
            recv_sem=hid_recv.at[c],
            device_id={"mp": peer},
            device_id_type=MESH,
        )

    def copy_block(o):
        at = pl.ds(o * block, block)
        return pltpu.make_async_remote_copy(
            src_ref=outbox.at[at],
            dst_ref=inbox.at[at],
            send_sem=a2a_send.at[o],
            recv_sem=a2a_recv.at[o],
            device_id={"dp": lax.rem(me + senders - order[o], senders)},
            device_id_type=MESH,
        )

    pick_tile = 128 * max(w for w in range(1, 9) if (d_vit // 128) % w == 0)
    chunk_rows = [of_chunk(c) for c in range(chunks)]
    norm_copy.wait_recv()

    def project(c):
        select = jnp.where(iota((CHUNK, rows), 1) == chunk_rows[c][0], 1.0, 0.0).astype(BF16)

        @pl.loop(0, d_vit // pick_tile)
        def _(j):
            cols = pl.ds(pl.multiple_of(j * pick_tile, pick_tile), pick_tile)
            picked[:, cols] = jnp.dot(
                select, normed[:, cols], preferred_element_type=F32
            ).astype(BF16)

        @pl.loop(0, tiles1)
        def _(j):
            if c == 0:
                w1_copy(j).wait()
            cols = pl.ds(pl.multiple_of(j * COL_TILE, COL_TILE), COL_TILE)
            pre = jnp.dot(picked[...], w1[:, cols], preferred_element_type=F32)
            pre = pre + proj_bias[:, cols].astype(F32)
            hidden[core, pl.ds(c * CHUNK, CHUNK), cols] = gelu(pre).astype(BF16)

        copy_hidden(c).start()

    q_at = iota((QUERY_PER_KEY * TILE, TILE), 0) % TILE
    s_at = iota((QUERY_PER_KEY * TILE, TILE), 1)
    allowed = (q_at // img_most == s_at // img_most) & (s_at <= q_at)

    def finish(c):
        copy_hidden(c).wait_recv()
        pos_hot = jnp.where(iota((CHUNK, TILE), 1) == chunk_rows[c][1], 1.0, 0.0).astype(BF16)
        terms = jnp.dot(pos_hot, table[...], preferred_element_type=F32)
        w = HEAD_SIZE
        cos = terms[:, :w] + terms[:, w : 2 * w] + terms[:, 2 * w : 3 * w]
        sin = terms[:, 3 * w : 4 * w] + terms[:, 4 * w : 5 * w] + terms[:, 5 * w :]

        @pl.loop(0, CHUNK // 16)
        def _(r):
            at = pl.ds(pl.multiple_of(c * CHUNK + r * 16, 16), 16)
            to = pl.ds(pl.multiple_of(r * 16, 16), 16)
            total = jnp.zeros((16, 1), F32)
            for h in range(2):
                x = hidden[h, at, :].astype(F32)
                total = total + jnp.sum(x * x, axis=-1, keepdims=True)
            scale = lax.rsqrt(total * (1.0 / (2 * half_cols)) + rms_epsilon)
            for h in range(2):
                x = hidden[h, at, :].astype(F32)
                g = rms_gain[:, h * half_cols : (h + 1) * half_cols].astype(F32)
                rms_normed[to, h * half_cols : (h + 1) * half_cols] = (x * scale * g).astype(BF16)

        @pl.loop(0, tiles2)
        def _(j):
            if c == 0:
                w2_copy(j).wait()
            cols = pl.ds(pl.multiple_of(j * COL_TILE, COL_TILE), COL_TILE)
            proj[:, cols] = jnp.dot(rms_normed[...], w2[:, cols], preferred_element_type=F32)

        def head(first, h, rotate):
            v = proj[first : first + TILE, h * w : (h + 1) * w]
            if rotate:
                v = v * cos[first : first + TILE] + pltpu.roll(v, w // 2, 1) * sin[first : first + TILE]
            return v.astype(BF16)

        for first in range(0, CHUNK, TILE):
            for g in range(groups):
                h0 = g * (QUERY_PER_KEY + 2)
                q = jnp.concatenate(
                    [head(first, h0 + i, True) for i in range(QUERY_PER_KEY)], axis=0
                )
                k = head(first, h0 + QUERY_PER_KEY, True)
                v = head(first, h0 + QUERY_PER_KEY + 1, False)
                scores = lax.dot_general(
                    q, k, (((1,), (1,)), ((), ())), preferred_element_type=F32
                ) * np.float32(HEAD_SIZE ** (-0.5))
                scores = jnp.where(allowed, scores, -1e30)
                weights = jnp.exp(scores - jnp.max(scores, axis=-1, keepdims=True))
                probs = (weights / jnp.sum(weights, axis=-1, keepdims=True)).astype(BF16)
                got = jnp.dot(probs, v, preferred_element_type=F32).astype(BF16)
                for i in range(QUERY_PER_KEY):
                    a = (g * QUERY_PER_KEY + i) * w
                    outbox[c * CHUNK + first : c * CHUNK + first + TILE, a : a + w] = got[
                        i * TILE : (i + 1) * TILE
                    ]
        for o in range(c * CHUNK // block, (c + 1) * CHUNK // block):
            if o < senders - 1:
                copy_block(o).start()
        if c == chunks - 1:
            inbox[box_rows - block :, :] = outbox[box_rows - block :, :]

    for c in range(chunks):
        project(c)
        if c > 0:
            finish(c - 1)
    finish(chunks - 1)

    t_at = iota((TILE, images), 0)
    image_at = iota((TILE, images), 1)
    place_of = []
    for t in range(tiles_dev):
        hit = (image_at // img_tile == t) & (t_at >= my_off_row) & (t_at < my_off_row + my_row)
        at = jnp.where(hit, slot_row * img_most + (t_at - my_off_row) + 1, 0)
        place_of.append(lane_sum(at) - 1)

    for o in range(senders - 1):
        copy_block(o).wait_recv()
    for t in range(tiles_dev):
        select = jnp.where(iota((TILE, box_rows), 1) == place_of[t], 1.0, 0.0).astype(BF16)
        out[t * TILE : (t + 1) * TILE, :] = jnp.dot(
            select, inbox[...], preferred_element_type=F32
        ).astype(BF16)

    norm_copy.wait_send()
    for c in range(chunks):
        copy_hidden(c).wait_send()
    for o in range(senders - 1):
        copy_block(o).wait_send()


def local(
    patches, ln_gain, ln_bias, w_proj, proj_bias, rms_gain, w_qkv, image_counts, source_shift
):
    senders = lax.axis_size("dp")
    order = shift_order(senders)
    half, d_vit = patches.shape
    rows = 2 * half
    half_cols = w_proj.shape[1]
    qkv_cols = w_qkv.shape[1]
    groups = qkv_cols // ((QUERY_PER_KEY + 2) * HEAD_SIZE)
    out_cols = groups * QUERY_PER_KEY * HEAD_SIZE
    images = source_shift.shape[0]
    img_most = TILE // (images // (rows // TILE))
    pair_slots = (images + senders - 1) // senders
    box_rows = senders * pair_slots * img_most
    chunks = box_rows // CHUNK
    vmem = pl.BlockSpec(memory_space=pltpu.VMEM)
    hbm = pl.BlockSpec(memory_space=pl.ANY)
    dma = pltpu.SemaphoreType.DMA
    return pl.pallas_call(
        functools.partial(kernel, senders, order),
        out_shape=jax.ShapeDtypeStruct((rows, out_cols), BF16),
        in_specs=[vmem] * 8 + [hbm] * 2,
        out_specs=vmem,
        scratch_shapes=[
            pltpu.VMEM(w_proj.shape, BF16),
            pltpu.VMEM(w_qkv.shape, BF16),
            pltpu.VMEM((rows, d_vit), BF16),
            pltpu.VMEM((CHUNK, d_vit), BF16),
            pltpu.VMEM((2, box_rows, half_cols), BF16),
            pltpu.VMEM((CHUNK, 2 * half_cols), BF16),
            pltpu.VMEM((CHUNK, qkv_cols), F32),
            pltpu.VMEM((box_rows, out_cols), BF16),
            pltpu.VMEM((box_rows, out_cols), BF16),
            dma((half_cols // COL_TILE,)),
            dma((qkv_cols // COL_TILE,)),
            dma((2,)),
            dma((chunks,)),
            dma((chunks,)),
            dma((senders,)),
            dma((senders,)),
        ],
        compiler_params=pltpu.CompilerParams(
            collective_id=0, has_side_effects=True, vmem_limit_bytes=60 * 1024 * 1024
        ),
        name="projector_attention",
    )(
        patches,
        ln_gain.reshape(1, -1),
        ln_bias.reshape(1, -1),
        proj_bias.reshape(1, -1),
        rms_gain.reshape(1, -1),
        image_counts.reshape(senders, images),
        source_shift.reshape(images, 1),
        jnp.asarray(rotary_parts()),
        w_proj,
        w_qkv,
    )


def solution(mesh):
    in_specs = (
        P(("dp", "mp"), None),
        P(),
        P(),
        P(None, "mp"),
        P("mp"),
        P(),
        P(None, "mp"),
        P(),
        P(),
    )
    out_specs = P("dp", "mp")
    return jax.shard_map(local, mesh=mesh, in_specs=in_specs, out_specs=out_specs, check_vma=False)
```

time: 171 us -> 73.1 us (0.43)
  waiting for transfers between devices: 69.1 us -> 0 us
  Pallas kernels: 0 us -> 62.5 us
  matrix products: 34.8 us -> 0 us
  other arithmetic: 23 us -> 0 us
  between operations: 13.7 us -> 0.01 us
  local copies, waits for them, and re-layouts: 23 us -> 10.3 us
  starting transfers between devices: 7.05 us -> 0 us
    pallas_call x0 -> x1, Pallas kernels: none -> 62.5 us  [local(): pl.pallas_call(functools.partial(kernel, senders, order), out_shape=jax.S...]
    all_to_all x1 -> x0, waiting for transfers between devices: 39.7 us -> none  [deliver(): lax.all_to_all(outbox.reshape(senders, pair_slots * img_most, blocks.shap...]
    dot_general x3 -> x0, matrix products: 31.5 us -> none  [the longest x1 19.8 us: local(): jnp.dot(normed, w_proj, preferred_element_type=jnp.float32)]
    all_gather x2 -> x0, waiting for transfers between devices: 29.4 us -> none  [the longest x1 15.8 us: local(): hidden = lax.all_gather(hidden_half, 'mp', axis=1, tiled=True)]
    gather x5 -> x0, local copies, waits for them, and re-layouts: 12.1 us -> none  [the longest x1 3.35 us: local(): jnp.take(projected, pick_rows, axis=0)]
    select_n x6 -> x0, other arithmetic: 8.07 us -> none  [the longest x1 3.26 us: local(): hidden_half = jnp.where(live_flat[:, None], placed, jnp.zeros_like(placed))]
    reduce_sum x5 -> x0, other arithmetic: 7.34 us -> none  [the longest x1 3.23 us: finish(): mean_square = jnp.mean(widened * widened, axis=-1, keepdims=True)]
    reshape x1 -> x6, local copies, waits for them, and re-layouts: 0.07 us -> 7.22 us  [the longest x1 1.33 us: local(): source_shift.reshape(images, 1)]
  transfers between devices with their start and end apart: 3 -> 0, of which waited for: 3 -> 0; matrix products, arithmetic and copies ran while one was open for 4% -> 0% of each run, Pallas kernels for 0% -> 0%
where the time goes in v1:
time: 73.1 us; the launch traced here: 72.7 us
  Pallas kernels  62.5 us (85%)
  local copies, waits for them, and re-layouts  10.3 us (14%)
    pallas_call x1, Pallas kernels, local(): pl.pallas_call(functools.partial(kernel, senders, order), out_shape=jax.S...  62.5 us
    unnamed x2, local copies, waits for them, and re-layouts  3.03 us

profile of v1, /device:TPU:0, one launch (start us, length us, event | category | flops | bytes accessed | tf_op | source)
XLA Modules:
  0.0 72.7 jit_solution(10069383094055566516)
XLA Ops:
  0.0 1.3 %reshape.20.proj_bias = bf16[1,2048]{1,0:T(2,128)(2,1)} reshape(bf16[2048]{0:T(1024)(128)(2,1)} %param.14) | data formatting | bytes 8192 | tf_op jit(solution)/shard_map/reshape | solution.py:387
  1.3 1.3 %reshape.18.ln_gain = bf16[1,3200]{1,0:T(2,128)(2,1)} reshape(bf16[3200]{0:T(1024)(128)(2,1)} %param.11) | data formatting | bytes 12800 | tf_op jit(solution)/shard_map/reshape | solution.py:385
  2.6 1.3 %reshape.19.ln_bias = bf16[1,3200]{1,0:T(2,128)(2,1)} reshape(bf16[3200]{0:T(1024)(128)(2,1)} %param.12) | data formatting | bytes 12800 | tf_op jit(solution)/shard_map/reshape | solution.py:386
  3.9 1.3 %reshape.21.rms_gain = bf16[1,4096]{1,0:T(2,128)(2,1)} reshape(bf16[4096]{0:T(1024)(128)(2,1)} %param.15) | data formatting | bytes 16384 | tf_op jit(solution)/shard_map/reshape | solution.py:388
  5.2 1.3 %copy.14.shift_col = s32[32,1]{1,0:T(8,128)} copy(s32[32,1]{0,1:T(1,128)} %bitcast.1) | data formatting | bytes 256 | tf_op jit(solution)/shard_map/reshape | solution.py:390
  6.5 0.8 %copy.13 = s32[64,8]{1,0:T(8,128)S(1)} copy(s32[64,8]{0,1:T(8,128)} %param.17) | data formatting | bytes 4096 | tf_op args[7]
  7.3 0.7 reshape.22.per_dest
  8.0 62.5 %projector_attention.1 = bf16[512,1024]{1,0:T(8,128)(2,1)} custom-call(bf16[256,3200]{1,0:T(8,128)(2,1)} %patches.1, bf16[1,3200]{1,0:T(2,128)(2,1)} %reshape.18.ln_gain, bf16[1,3200]{1,0:T(2,128)(2,1)} %reshape.19.ln_bias, bf16[1,2048]{1,0:T(2,128)(2,1)} %reshape.20.proj_bias, bf16[1,4096]{1,0:T(2,128)(2,1)} %reshape.21.rms_gain, ...), custom_call_target="tpu_custom_call" | custom-call | tf_op jit(solution)/shard_map/projector_attention/pallas_call | solution.py:356
  70.5 2.3 %copy.16 = bf16[512,1024]{1,0:T(8,128)(2,1)} copy(bf16[512,1024]{1,0:T(8,128)(2,1)} %projector_attention.1) | data formatting | bytes 2097152

commit v2 on v1

v2 whole, which is shorter than its diff:
```python
import functools

import jax
import jax.numpy as jnp
import numpy as np
from jax import lax
from jax.experimental import pallas as pl
from jax.experimental.pallas import tpu as pltpu
from jax.sharding import PartitionSpec as P

HEAD_SIZE = 128
TILE = 128
QUERY_PER_KEY = 4
COL_TILE = 256
CHUNKS = (256, 256)

norm_epsilon = 1e-05
rms_epsilon = 1e-05
rotary_base = 500000.0

F32 = jnp.float32
BF16 = jnp.bfloat16
MESH = pl.DeviceIdType.MESH


def shift_order(senders):
    return sorted(range(senders), key=lambda v: (abs(v - senders // 2), v))


def rotary_parts():
    frequency = np.float32(rotary_base) ** (
        -(np.arange(HEAD_SIZE // 2, dtype=np.float32) * np.float32(2.0 / HEAD_SIZE))
    )
    angles = np.arange(TILE, dtype=np.float32)[:, None] * frequency[None, :].astype(np.float32)
    cos = np.cos(angles.astype(np.float64)).astype(np.float32)
    sin = np.sin(angles.astype(np.float64)).astype(np.float32)
    parts = []
    for table in (np.concatenate([cos, cos], 1), np.concatenate([-sin, sin], 1)):
        rest = table
        for _ in range(3):
            term = rest.astype(jnp.bfloat16)
            parts.append(term)
            rest = rest - term.astype(np.float32)
    return np.concatenate(parts, axis=1)


def chunk_list(box_rows):
    sizes = list(CHUNKS)
    while sum(sizes) < box_rows:
        sizes.append(CHUNKS[-1])
    return sizes


def gelu(v):
    return 0.5 * v * (1.0 + lax.erf(v * np.float32(0.5**0.5)))


def iota(shape, axis):
    return lax.broadcasted_iota(jnp.int32, shape, axis)


def lane_sum(x):
    return jnp.sum(x, axis=1, keepdims=True)


def kernel(
    senders,
    order,
    ln_gain,
    ln_bias,
    proj_bias,
    rms_gain,
    counts,
    source_shift,
    table,
    patches,
    w_proj,
    w_qkv,
    out,
    raw,
    w1,
    w2,
    normed,
    picked,
    hidden,
    rms_normed,
    pre,
    bias,
    proj,
    outbox,
    inbox,
    placed,
    raw_sem,
    out_sem,
    w1_sem,
    w2_sem,
    norm_send,
    norm_recv,
    hid_send,
    hid_recv,
    a2a_send,
    a2a_recv,
):
    me = lax.axis_index("dp")
    core = lax.axis_index("mp")
    peer = 1 - core
    half, d_vit = raw.shape
    rows = 2 * half
    box_rows = outbox.shape[0]
    block = box_rows // senders
    images = source_shift.shape[0]
    tiles_dev = rows // TILE
    img_tile = images // tiles_dev
    img_most = TILE // img_tile
    pair_slots = block // img_most
    sizes = chunk_list(box_rows)
    chunks = len(sizes)
    firsts = [sum(sizes[:c]) for c in range(chunks)]
    half_cols = w_proj.shape[1]
    qkv_cols = w_qkv.shape[1]
    groups = qkv_cols // ((QUERY_PER_KEY + 2) * HEAD_SIZE)
    tiles1 = half_cols // COL_TILE
    tiles2 = qkv_cols // COL_TILE

    part = half // 2

    def raw_copy(i):
        at = pl.ds(i * part, part)
        return pltpu.make_async_copy(patches.at[at], raw.at[at], raw_sem.at[i])

    for i in range(2):
        raw_copy(i).start()

    barrier = pltpu.get_barrier_semaphore()
    pl.semaphore_signal(barrier, inc=1, device_id={"mp": peer}, device_id_type=MESH)
    for v in range(1, senders):
        pl.semaphore_signal(
            barrier, inc=1, device_id={"dp": lax.rem(me + v, senders)}, device_id_type=MESH
        )

    def w1_copy(j):
        cols = pl.ds(pl.multiple_of(j * COL_TILE, COL_TILE), COL_TILE)
        return pltpu.make_async_copy(w_proj.at[:, cols], w1.at[:, cols], w1_sem.at[j])

    def w2_copy(j):
        cols = pl.ds(pl.multiple_of(j * COL_TILE, COL_TILE), COL_TILE)
        return pltpu.make_async_copy(w_qkv.at[:, cols], w2.at[:, cols], w2_sem.at[j])

    gain_f = ln_gain[...].reshape(1, -1).astype(F32)
    bias_f = ln_bias[...].reshape(1, -1).astype(F32)

    def norm_copy(i):
        mine = normed.at[pl.ds(pl.multiple_of(core * half + i * part, part), part)]
        return pltpu.make_async_remote_copy(
            src_ref=mine,
            dst_ref=mine,
            send_sem=norm_send.at[i],
            recv_sem=norm_recv.at[i],
            device_id={"mp": peer},
            device_id_type=MESH,
        )

    for i in range(2):
        raw_copy(i).wait()
        if i == 0:
            for j in range(tiles1):
                w1_copy(j).start()
            for j in range(tiles2):
                w2_copy(j).start()

        @pl.loop(0, part // 16, unroll=2)
        def _(r):
            values = raw[pl.ds(pl.multiple_of(i * part + r * 16, 16), 16), :].astype(F32)
            centred = values - jnp.mean(values, axis=-1, keepdims=True)
            variance = jnp.mean(centred * centred, axis=-1, keepdims=True)
            scaled = centred * lax.rsqrt(variance + norm_epsilon) * gain_f + bias_f
            to = pl.ds(pl.multiple_of(core * half + i * part + r * 16, 16), 16)
            normed[to, :] = scaled.astype(BF16)

        if i == 0:
            pl.semaphore_wait(barrier, senders)
        norm_copy(i).start()

    sq = (images, images)
    k_at, l_at = iota(sq, 0), iota(sq, 1)
    eye = k_at == l_at
    before = l_at < k_at
    same_tile = (k_at // img_tile) == (l_at // img_tile)

    def to_row(col):
        return jnp.sum(jnp.where(eye, col, 0), axis=0, keepdims=True)

    tiles_all = counts.shape[1]
    spread = (iota((img_tile, images), 1) % img_tile == iota((img_tile, images), 0)).astype(F32)
    wide = lax.dot_general(
        counts[...].astype(F32).astype(BF16),
        spread.astype(BF16),
        (((0,), (0,)), ((), ())),
        preferred_element_type=F32,
    )
    own_tile = iota((tiles_all, images), 1) // img_tile == iota((tiles_all, images), 0) % tiles_dev
    wide = jnp.where(own_tile, wide, 0.0).astype(BF16)
    gather = (iota((senders, tiles_all), 1) // tiles_dev == iota((senders, tiles_all), 0)).astype(F32)
    per_dest = jnp.dot(gather.astype(BF16), wide, preferred_element_type=F32).astype(jnp.int32)

    shift_row = source_shift[...].reshape(1, images)
    shift = lane_sum(jnp.where(eye, shift_row, 0))
    dest = me - shift
    dest = jnp.where(dest < 0, dest + senders, dest)
    counts_to = jnp.zeros(sq, jnp.int32)
    place = jnp.zeros((images, 1), jnp.int32)
    for v in range(senders):
        counts_to = jnp.where(dest == v, per_dest[v : v + 1, :], counts_to)
        place = jnp.where(shift == order[v], v, place)
    sent_row = jnp.sum(jnp.where(eye, counts_to, 0), axis=0, keepdims=True)
    starts = lane_sum(jnp.where(before, sent_row, 0))
    far_offset = lane_sum(jnp.where(before & same_tile, counts_to, 0))
    rank = lane_sum(jnp.where(before & (shift_row == shift), 1, 0))
    slot_row = to_row(place * pair_slots + rank)
    starts_row = to_row(starts)
    far_row = to_row(far_offset)

    dest_at = iota(per_dest.shape, 0)
    my_row = jnp.sum(jnp.where(dest_at == me, per_dest, 0), axis=0, keepdims=True)
    my_offset = lane_sum(jnp.where(before & same_tile, my_row, 0))
    my_off_row = to_row(my_offset)

    def of_chunk(c):
        row_at = iota((sizes[c], images), 0) + firsts[c]
        hit = slot_row == row_at // img_most
        inside = iota((sizes[c], 1), 0) % img_most
        src = lane_sum(jnp.where(hit, starts_row, 0)) + inside
        pos = lane_sum(jnp.where(hit, far_row, 0)) + inside
        return src, pos

    def copy_hidden(c, part):
        ref = hidden.at[
            core, pl.ds(firsts[c], sizes[c]), pl.ds(part * half_cols // 2, half_cols // 2)
        ]
        return pltpu.make_async_remote_copy(
            src_ref=ref,
            dst_ref=ref,
            send_sem=hid_send.at[2 * c + part],
            recv_sem=hid_recv.at[2 * c + part],
            device_id={"mp": peer},
            device_id_type=MESH,
        )

    def copy_block(o):
        at = pl.ds(o * block, block)
        return pltpu.make_async_remote_copy(
            src_ref=outbox.at[at],
            dst_ref=inbox.at[at],
            send_sem=a2a_send.at[o],
            recv_sem=a2a_recv.at[o],
            device_id={"dp": lax.rem(me + senders - order[o], senders)},
            device_id_type=MESH,
        )

    pick_tile = 128 * max(w for w in range(1, 9) if (d_vit // 128) % w == 0)
    chunk_rows = [of_chunk(c) for c in range(chunks)]
    for i in range(2):
        norm_copy(i).wait_recv()

    def project(c):
        size = sizes[c]
        rows_at = pl.ds(firsts[c], size)
        select = jnp.where(iota((size, rows), 1) == chunk_rows[c][0], 1.0, 0.0).astype(BF16)

        @pl.loop(0, d_vit // pick_tile)
        def _(j):
            cols = pl.ds(pl.multiple_of(j * pick_tile, pick_tile), pick_tile)
            picked[:size, cols] = jnp.dot(
                select, normed[:, cols], preferred_element_type=F32
            ).astype(BF16)

        def columns(j):
            return pl.ds(pl.multiple_of(j * COL_TILE, COL_TILE), COL_TILE)

        def multiply(j, slot):
            if c == 0:
                w1_copy(j).wait()
            pre[slot, :size] = jnp.dot(
                picked[:size], w1[:, columns(j)], preferred_element_type=F32
            )

        bias_row = proj_bias[...].reshape(1, -1)

        def activate(j, slot):
            x = pre[slot, :size] + bias[:, columns(j)]
            hidden[core, rows_at, columns(j)] = gelu(x).astype(BF16)

        if c == 0:
            bias[...] = bias_row.astype(F32)
        multiply(0, 0)
        pairs = tiles1 // 2
        for part in range(2):
            low, high = part * pairs // 2, (part + 1) * pairs // 2 - part

            @pl.loop(low, high)
            def _(i):
                multiply(2 * i + 1, 1)
                activate(2 * i, 0)
                multiply(2 * i + 2, 0)
                activate(2 * i + 1, 1)

            if part == 1:
                multiply(tiles1 - 1, 1)
                activate(tiles1 - 2, 0)
                activate(tiles1 - 1, 1)
            copy_hidden(c, part).start()

    q_at = iota((QUERY_PER_KEY * TILE, TILE), 0) % TILE
    s_at = iota((QUERY_PER_KEY * TILE, TILE), 1)
    allowed = (q_at // img_most == s_at // img_most) & (s_at <= q_at)

    def finish(c):
        size = sizes[c]
        for part in range(2):
            copy_hidden(c, part).wait_recv()
        pos_hot = jnp.where(iota((size, TILE), 1) == chunk_rows[c][1], 1.0, 0.0).astype(BF16)
        terms = jnp.dot(pos_hot, table[...], preferred_element_type=F32)
        w = HEAD_SIZE
        cos = terms[:, :w] + terms[:, w : 2 * w] + terms[:, 2 * w : 3 * w]
        sin = terms[:, 3 * w : 4 * w] + terms[:, 4 * w : 5 * w] + terms[:, 5 * w :]

        gains = rms_gain[...].reshape(1, -1).astype(F32)

        @pl.loop(0, size // 16, unroll=2)
        def _(r):
            at = pl.ds(pl.multiple_of(firsts[c] + r * 16, 16), 16)
            to = pl.ds(pl.multiple_of(r * 16, 16), 16)
            total = jnp.zeros((16, 1), F32)
            for h in range(2):
                x = hidden[h, at, :].astype(F32)
                total = total + jnp.sum(x * x, axis=-1, keepdims=True)
            scale = lax.rsqrt(total * (1.0 / (2 * half_cols)) + rms_epsilon)
            for h in range(2):
                x = hidden[h, at, :].astype(F32)
                g = gains[:, h * half_cols : (h + 1) * half_cols]
                rms_normed[to, h * half_cols : (h + 1) * half_cols] = (x * scale * g).astype(BF16)

        @pl.loop(0, tiles2)
        def _(j):
            if c == 0:
                w2_copy(j).wait()
            cols = pl.ds(pl.multiple_of(j * COL_TILE, COL_TILE), COL_TILE)
            proj[:size, cols] = jnp.dot(rms_normed[:size], w2[:, cols], preferred_element_type=F32)

        def head(first, h, rotate):
            v = proj[first : first + TILE, h * w : (h + 1) * w]
            if rotate:
                v = v * cos[first : first + TILE] + pltpu.roll(v, w // 2, 1) * sin[first : first + TILE]
            return v.astype(BF16)

        for first in range(0, size, TILE):
            for g in range(groups):
                h0 = g * (QUERY_PER_KEY + 2)
                q = jnp.concatenate(
                    [head(first, h0 + i, True) for i in range(QUERY_PER_KEY)], axis=0
                )
                k = head(first, h0 + QUERY_PER_KEY, True)
                v = head(first, h0 + QUERY_PER_KEY + 1, False)
                scores = lax.dot_general(
                    q, k, (((1,), (1,)), ((), ())), preferred_element_type=F32
                ) * np.float32(HEAD_SIZE ** (-0.5))
                scores = jnp.where(allowed, scores, -1e30)
                weights = jnp.exp(scores - jnp.max(scores, axis=-1, keepdims=True))
                probs = (weights / jnp.sum(weights, axis=-1, keepdims=True)).astype(BF16)
                got = jnp.dot(probs, v, preferred_element_type=F32).astype(BF16)
                for i in range(QUERY_PER_KEY):
                    a = (g * QUERY_PER_KEY + i) * w
                    outbox[firsts[c] + first : firsts[c] + first + TILE, a : a + w] = got[
                        i * TILE : (i + 1) * TILE
                    ]
        for o in range(firsts[c] // block, (firsts[c] + size) // block):
            if o < senders - 1:
                copy_block(o).start()
        if c == chunks - 1:
            inbox[box_rows - block :, :] = outbox[box_rows - block :, :]

    for c in range(chunks):
        project(c)
        finish(c)

    t_at = iota((TILE, images), 0)
    image_at = iota((TILE, images), 1)
    place_of = []
    for t in range(tiles_dev):
        hit = (image_at // img_tile == t) & (t_at >= my_off_row) & (t_at < my_off_row + my_row)
        at = jnp.where(hit, slot_row * img_most + (t_at - my_off_row) + 1, 0)
        place_of.append(lane_sum(at) - 1)

    def out_copy(t):
        at = pl.ds(t * TILE, TILE)
        return pltpu.make_async_copy(placed.at[at], out.at[at], out_sem.at[t])

    for o in range(senders - 1):
        copy_block(o).wait_recv()
    for t in range(tiles_dev):
        select = jnp.where(iota((TILE, box_rows), 1) == place_of[t], 1.0, 0.0).astype(BF16)
        placed[t * TILE : (t + 1) * TILE, :] = jnp.dot(
            select, inbox[...], preferred_element_type=F32
        ).astype(BF16)
        out_copy(t).start()
    for t in range(tiles_dev):
        out_copy(t).wait()

    for i in range(2):
        norm_copy(i).wait_send()
    for c in range(chunks):
        for part in range(2):
            copy_hidden(c, part).wait_send()
    for o in range(senders - 1):
        copy_block(o).wait_send()


def local(
    patches, ln_gain, ln_bias, w_proj, proj_bias, rms_gain, w_qkv, image_counts, source_shift
):
    senders = lax.axis_size("dp")
    order = shift_order(senders)
    half, d_vit = patches.shape
    rows = 2 * half
    half_cols = w_proj.shape[1]
    qkv_cols = w_qkv.shape[1]
    groups = qkv_cols // ((QUERY_PER_KEY + 2) * HEAD_SIZE)
    out_cols = groups * QUERY_PER_KEY * HEAD_SIZE
    images = source_shift.shape[0]
    img_most = TILE // (images // (rows // TILE))
    pair_slots = (images + senders - 1) // senders
    box_rows = senders * pair_slots * img_most
    sizes = chunk_list(box_rows)
    chunks = len(sizes)
    size = max(sizes)
    vmem = pl.BlockSpec(memory_space=pltpu.VMEM)
    hbm = pl.BlockSpec(memory_space=pl.ANY)
    dma = pltpu.SemaphoreType.DMA
    return pl.pallas_call(
        functools.partial(kernel, senders, order),
        out_shape=jax.ShapeDtypeStruct((rows, out_cols), BF16),
        in_specs=[vmem] * 7 + [hbm] * 3,
        out_specs=hbm,
        scratch_shapes=[
            pltpu.VMEM((half, d_vit), BF16),
            pltpu.VMEM(w_proj.shape, BF16),
            pltpu.VMEM(w_qkv.shape, BF16),
            pltpu.VMEM((rows, d_vit), BF16),
            pltpu.VMEM((size, d_vit), BF16),
            pltpu.VMEM((2, box_rows, half_cols), BF16),
            pltpu.VMEM((size, 2 * half_cols), BF16),
            pltpu.VMEM((2, size, COL_TILE), F32),
            pltpu.VMEM((1, half_cols), F32),
            pltpu.VMEM((size, qkv_cols), F32),
            pltpu.VMEM((box_rows, out_cols), BF16),
            pltpu.VMEM((box_rows, out_cols), BF16),
            pltpu.VMEM((rows, out_cols), BF16),
            dma((2,)),
            dma((rows // TILE,)),
            dma((half_cols // COL_TILE,)),
            dma((qkv_cols // COL_TILE,)),
            dma((2,)),
            dma((2,)),
            dma((2 * chunks,)),
            dma((2 * chunks,)),
            dma((senders,)),
            dma((senders,)),
        ],
        compiler_params=pltpu.CompilerParams(
            collective_id=0, has_side_effects=True, vmem_limit_bytes=60 * 1024 * 1024
        ),
        name="projector_attention",
    )(
        ln_gain,
        ln_bias,
        proj_bias,
        rms_gain,
        image_counts.T,
        source_shift,
        jnp.asarray(rotary_parts()),
        patches,
        w_proj,
        w_qkv,
    )


def solution(mesh):
    in_specs = (
        P(("dp", "mp"), None),
        P(),
        P(),
        P(None, "mp"),
        P("mp"),
        P(),
        P(None, "mp"),
        P(),
        P(),
    )
    out_specs = P("dp", "mp")
    return jax.shard_map(local, mesh=mesh, in_specs=in_specs, out_specs=out_specs, check_vma=False)
```

time: 73.1 us -> 59.9 us (0.82)
  local copies, waits for them, and re-layouts: 10.3 us -> 2.26 us
  Pallas kernels: 62.5 us -> 57.5 us
    reshape x6 -> x0, local copies, waits for them, and re-layouts: 7.22 us -> none  [the longest x1 1.33 us: local(): source_shift.reshape(images, 1)]
    pallas_call x1, Pallas kernels: 62.5 us -> 57.5 us  [local(): pl.pallas_call(functools.partial(kernel, senders, order), out_shape=jax.S...]
    unnamed x2 -> x1, local copies, waits for them, and re-layouts: 3.03 us -> 2.26 us
where the time goes in v2:
time: 59.9 us; the launch traced here: 59.7 us
  Pallas kernels  57.5 us (96%)
  local copies, waits for them, and re-layouts  2.26 us (4%)
    pallas_call x1, Pallas kernels, local(): pl.pallas_call(functools.partial(kernel, senders, order), out_shape=jax.S...  57.5 us
    unnamed x1, local copies, waits for them, and re-layouts  2.26 us

profile of v2, /device:TPU:0, one launch (start us, length us, event | category | flops | bytes accessed | tf_op | source)
XLA Modules:
  0.0 59.7 jit_solution(14662054428260556923)
XLA Ops:
  0.0 57.5 %projector_attention.1 = bf16[512,1024]{1,0:T(8,128)(2,1)} custom-call(bf16[3200]{0:T(1024)(128)(2,1)} %ln_gain.1, bf16[3200]{0:T(1024)(128)(2,1)} %ln_bias.1, bf16[2048]{0:T(1024)(128)(2,1)} %proj_bias.1, bf16[4096]{0:T(1024)(128)(2,1)} %rms_gain.1, s32[8,64]{1,0:T(8,128)} %bitcast.1, s32[32]{0:T(128)} %source_shift.1, ...), custom_call_target="tpu_custom_call" | custom-call | tf_op jit(solution)/shard_map/projector_attention/pallas_call | solution.py:439
  57.5 2.3 %copy.12 = bf16[512,1024]{1,0:T(8,128)(2,1)} copy(bf16[512,1024]{1,0:T(8,128)(2,1)} %projector_attention.1) | data formatting | bytes 2097152
